TPU v7x, 32 devices: a whole 2x2x4 slice. The times are simulated.
32 devices in a mesh: dp: 8 (over z, x), head: 4 (over y, core).
Axes of the slice: x: 2, y: 2, z: 4, core: 2. Of those that a mesh axis runs over, the one named last changes fastest.
Arguments:
- inputs: bfloat16 [16384, 1024], P(('dp', 'head')), may hold values from -6 to 6
- lengths: int32 [8, 4], P('dp'), may hold values from 1 to 1024, 2048 in all within a row
- attn_gain: bfloat16 [1024], replicated, may hold values from 0.5 to 1.5
- attn_shift: bfloat16 [1024], replicated, may hold values from -3 to 3
- mlp_gain: bfloat16 [1024], replicated, may hold values from 0.5 to 1.5
- mlp_shift: bfloat16 [1024], replicated, may hold values from -3 to 3
- w_qkv: bfloat16 [1024, 3072], replicated, may hold values from -0.1875 to 0.1875
- b_qkv: bfloat16 [3072], replicated, may hold values from -3 to 3
- w_out: bfloat16 [1024, 1024], replicated, may hold values from -1.5 to 1.5
- b_out: bfloat16 [1024], replicated, may hold values from -3 to 3
- w_up: bfloat16 [1024, 4096], replicated, may hold values from -0.1875 to 0.1875
- b_up: bfloat16 [4096], replicated, may hold values from -3 to 3
- w_down: bfloat16 [4096, 1024], replicated, may hold values from -0.09375 to 0.09375
- b_down: bfloat16 [1024], replicated, may hold values from -3 to 3
- cotangent: bfloat16 [16384, 1024], P(('dp', 'head')), may hold values from -6 to 6
Outputs:
- output: bfloat16 [16384, 1024], P(('dp', 'head'))
- grad_inputs: float32 [16384, 1024], P(('dp', 'head'))
- grad_attn_gain: float32 [1024], replicated
- grad_attn_shift: float32 [1024], replicated
- grad_mlp_gain: float32 [1024], replicated
- grad_mlp_shift: float32 [1024], replicated
- grad_w_qkv: float32 [1024, 3072], P('dp', 'head')
- grad_b_qkv: float32 [3072], replicated
- grad_w_out: float32 [1024, 1024], P('dp', 'head')
- grad_b_out: float32 [1024], replicated
- grad_w_up: float32 [1024, 4096], P('dp', 'head')
- grad_b_up: float32 [4096], replicated
- grad_w_down: float32 [4096, 1024], P('dp', 'head')
- grad_b_down: float32 [1024], replicated
Inputs may be any that keep to these rules, and one draw needn't show every extreme that they name: Each row lists the lengths of the 4 sequences packed in order into one group of 2048 tokens; a row sums to 2048 and its longest sequence has 1024 tokens.
All inputs are finite; a program needn't handle non-finite values.
Results may differ from a plain program's by a relative error of at most 0.012.
Values may be sent and summed in bfloat16 or wider, within the bound.
A program may use at most 192 MiB of HBM per device.

v0:
```python
import jax
import jax.numpy as jnp
from jax import lax
from jax.sharding import PartitionSpec as P

HD = 64
ROT = 16


def layer_norm(value, gain, shift):
    center = value - jnp.mean(value, axis=-1, keepdims=True)
    scale_inv = lax.rsqrt(jnp.mean(center * center, axis=-1, keepdims=True) + 1e-05)
    normed = center * scale_inv
    return (normed * gain + shift, normed, scale_inv)


def norm_back(grad_norm, normed, scale_inv, gain):
    grad_hat = grad_norm * gain
    grad_value = scale_inv * (
        grad_hat
        - jnp.mean(grad_hat, axis=-1, keepdims=True)
        - normed * jnp.mean(grad_hat * normed, axis=-1, keepdims=True)
    )
    return (grad_value, jnp.sum(grad_norm * normed, axis=0), jnp.sum(grad_norm, axis=0))


def group_layout(seq_lens, total_len):
    seq_ends = jnp.cumsum(seq_lens, dtype=jnp.int32)
    starts = seq_ends - seq_lens
    index = jnp.arange(total_len, dtype=jnp.int32)
    segment = jnp.sum(
        (index[:, None] >= seq_ends[None, :]).astype(jnp.int32), axis=1, dtype=jnp.int32
    )
    chosen = segment[:, None] == jnp.arange(seq_lens.shape[0], dtype=jnp.int32)[None, :]
    offset = jnp.sum(jnp.where(chosen, starts[None, :], 0), axis=1, dtype=jnp.int32)
    return (segment, index - offset)


def rotate(value, position, sign):
    half_rot = ROT // 2
    freqs = 10000.0 ** (-(2.0 * jnp.arange(half_rot, dtype=jnp.float32)) / ROT)
    angles = position.astype(jnp.float32)[:, None] * freqs[None, :]
    cosine = jnp.cos(angles)[:, None, :]
    sine = jnp.sin(angles)[:, None, :]
    first = value[..., :half_rot]
    second = value[..., half_rot:ROT]
    return jnp.concatenate(
        [
            first * cosine - sign * second * sine,
            second * cosine + sign * first * sine,
            value[..., ROT:],
        ],
        axis=-1,
    )


def block_scores(queries, keys_rot, segment, start, block):
    query_blk = lax.dynamic_slice_in_dim(queries, start, block, 0)
    row_seg = lax.dynamic_slice_in_dim(segment, start, block, 0)
    row_index = start + jnp.arange(block, dtype=jnp.int32)
    key_index = jnp.arange(keys_rot.shape[0], dtype=jnp.int32)
    scores = jnp.einsum(
        "qhd,khd->hqk", query_blk, keys_rot, preferred_element_type=jnp.float32
    ) * HD ** (-0.5)
    allowed = (row_seg[:, None] == segment[None, :]) & (key_index[None, :] <= row_index[:, None])
    return (jnp.where(allowed[None], scores, -1e30), query_blk)


def body(
    inputs,
    lengths,
    attn_gain,
    attn_shift,
    mlp_gain,
    mlp_shift,
    w_qkv,
    b_qkv,
    w_out,
    b_out,
    w_up,
    b_up,
    w_down,
    b_down,
    cotangent,
):
    tok_rows = inputs.shape[0]
    width = inputs.shape[1]
    in_float = inputs.astype(jnp.float32)
    gain_attn = attn_gain.astype(jnp.float32)
    gain_mlp = mlp_gain.astype(jnp.float32)
    norm_attn, normed_attn, inv_attn = layer_norm(
        in_float, gain_attn, attn_shift.astype(jnp.float32)
    )
    norm_mlp, normed_mlp, inv_mlp = layer_norm(in_float, gain_mlp, mlp_shift.astype(jnp.float32))
    norm_attn = norm_attn.astype(jnp.bfloat16)
    norm_mlp = norm_mlp.astype(jnp.bfloat16)
    triple = (
        jnp.dot(norm_attn, w_qkv, preferred_element_type=jnp.float32) + b_qkv.astype(jnp.float32)
    ).astype(jnp.bfloat16)
    triple_heads = lax.all_to_all(
        triple.reshape(tok_rows, 3, width), "head", split_axis=2, concat_axis=0, tiled=True
    )
    group_rows = triple_heads.shape[0]
    local_width = triple_heads.shape[2]
    local_heads = local_width // HD
    segment, position = group_layout(lengths[0], group_rows)
    queries = rotate(
        triple_heads[:, 0].astype(jnp.float32).reshape(group_rows, local_heads, HD), position, 1.0
    ).astype(jnp.bfloat16)
    keys_rot = rotate(
        triple_heads[:, 1].astype(jnp.float32).reshape(group_rows, local_heads, HD), position, 1.0
    ).astype(jnp.bfloat16)
    values = triple_heads[:, 2].reshape(group_rows, local_heads, HD)
    block = min(512, group_rows)
    blocks = group_rows // block

    def forward_block(block_id):
        scores, unused = block_scores(queries, keys_rot, segment, block_id * block, block)
        peak = jnp.max(scores, axis=-1, keepdims=True)
        weights = jnp.exp(scores - peak)
        totals = jnp.sum(weights, axis=-1, keepdims=True)
        probs = (weights / totals).astype(jnp.bfloat16)
        out_blk = jnp.einsum("hqk,khd->qhd", probs, values, preferred_element_type=jnp.float32)
        return (out_blk.astype(jnp.bfloat16), (peak + jnp.log(totals))[..., 0])

    context_blocks, log_totals = lax.map(forward_block, jnp.arange(blocks, dtype=jnp.int32))
    context_heads = context_blocks.reshape(group_rows, local_width)
    context = lax.all_to_all(context_heads, "head", split_axis=0, concat_axis=1, tiled=True)
    attn_part = jnp.dot(context, w_out, preferred_element_type=jnp.float32) + b_out.astype(
        jnp.float32
    )
    pre_act = jnp.dot(norm_mlp, w_up, preferred_element_type=jnp.float32) + b_up.astype(jnp.float32)
    gelu_value, gelu_pull = jax.vjp(lambda value: jax.nn.gelu(value, approximate=False), pre_act)
    hidden = gelu_value.astype(jnp.bfloat16)
    mlp_part = jnp.dot(hidden, w_down, preferred_element_type=jnp.float32) + b_down.astype(
        jnp.float32
    )
    output = (in_float + attn_part + mlp_part).astype(jnp.bfloat16)
    grad_float = cotangent.astype(jnp.float32)
    grad_w_down = jnp.einsum("tf,td->fd", hidden, cotangent, preferred_element_type=jnp.float32)
    grad_hidden = jnp.einsum("td,fd->tf", cotangent, w_down, preferred_element_type=jnp.float32)
    grad_pre = gelu_pull(grad_hidden)[0].astype(jnp.bfloat16)
    grad_w_up = jnp.einsum("td,tf->df", norm_mlp, grad_pre, preferred_element_type=jnp.float32)
    grad_norm_mlp = jnp.einsum("tf,df->td", grad_pre, w_up, preferred_element_type=jnp.float32)
    grad_w_out = jnp.einsum("td,te->de", context, cotangent, preferred_element_type=jnp.float32)
    grad_context = jnp.einsum(
        "te,de->td", cotangent, w_out, preferred_element_type=jnp.float32
    ).astype(jnp.bfloat16)
    grad_ctx_heads = lax.all_to_all(grad_context, "head", split_axis=1, concat_axis=0, tiled=True)
    grad_ctx_heads = grad_ctx_heads.reshape(group_rows, local_heads, HD)
    scale = HD ** (-0.5)

    def backward_block(carry, block_id):
        grad_keys, grad_values = carry
        start = block_id * block
        scores, query_blk = block_scores(queries, keys_rot, segment, start, block)
        probs = jnp.exp(scores - log_totals[block_id][:, :, None])
        probs_low = probs.astype(jnp.bfloat16)
        grad_out_blk = lax.dynamic_slice_in_dim(grad_ctx_heads, start, block, 0)
        grad_values = grad_values + jnp.einsum(
            "hqk,qhd->khd", probs_low, grad_out_blk, preferred_element_type=jnp.float32
        )
        grad_probs = jnp.einsum(
            "qhd,khd->hqk", grad_out_blk, values, preferred_element_type=jnp.float32
        )
        inner = jnp.sum(probs * grad_probs, axis=-1, keepdims=True)
        grad_scores = (probs * (grad_probs - inner)).astype(jnp.bfloat16)
        grad_query = (
            jnp.einsum("hqk,khd->qhd", grad_scores, keys_rot, preferred_element_type=jnp.float32)
            * scale
        )
        grad_keys = (
            grad_keys
            + jnp.einsum("hqk,qhd->khd", grad_scores, query_blk, preferred_element_type=jnp.float32)
            * scale
        )
        return ((grad_keys, grad_values), grad_query)

    zeros_kv = jnp.zeros((group_rows, local_heads, HD), jnp.float32)
    (grad_keys, grad_values), grad_queries = lax.scan(
        backward_block, (zeros_kv, zeros_kv), jnp.arange(blocks, dtype=jnp.int32)
    )
    grad_queries = rotate(grad_queries.reshape(group_rows, local_heads, HD), position, -1.0)
    grad_keys = rotate(grad_keys, position, -1.0)
    grad_heads = (
        jnp.stack([grad_queries, grad_keys, grad_values], axis=1)
        .reshape(group_rows, 3, local_width)
        .astype(jnp.bfloat16)
    )
    grad_triple = lax.all_to_all(
        grad_heads, "head", split_axis=0, concat_axis=2, tiled=True
    ).reshape(tok_rows, 3 * width)
    grad_w_qkv = jnp.einsum("td,te->de", norm_attn, grad_triple, preferred_element_type=jnp.float32)
    grad_norm_attn = jnp.einsum("te,de->td", grad_triple, w_qkv, preferred_element_type=jnp.float32)
    grad_x_attn, grad_gain_attn, grad_shift_attn = norm_back(
        grad_norm_attn, normed_attn, inv_attn, gain_attn
    )
    grad_x_mlp, grad_gain_mlp, grad_shift_mlp = norm_back(
        grad_norm_mlp, normed_mlp, inv_mlp, gain_mlp
    )
    grad_inputs = grad_float + grad_x_attn + grad_x_mlp
    column_sum = jnp.sum(grad_float, axis=0)
    summed = lax.psum(
        (
            grad_gain_attn,
            grad_shift_attn,
            grad_gain_mlp,
            grad_shift_mlp,
            jnp.sum(grad_triple.astype(jnp.float32), axis=0),
            column_sum,
            jnp.sum(grad_pre.astype(jnp.float32), axis=0),
        ),
        ("dp", "head"),
    )
    matrices = (grad_w_qkv, grad_w_out, grad_w_up, grad_w_down)
    partial_rows = (
        lax.psum_scatter(matrices[0], "dp", scatter_dimension=0, tiled=True),
        lax.psum_scatter(matrices[1], "dp", scatter_dimension=0, tiled=True),
        lax.psum_scatter(matrices[2], "dp", scatter_dimension=0, tiled=True),
        lax.psum_scatter(matrices[3], "dp", scatter_dimension=0, tiled=True),
    )
    finals = (
        lax.psum_scatter(partial_rows[0], "head", scatter_dimension=1, tiled=True),
        lax.psum_scatter(partial_rows[1], "head", scatter_dimension=1, tiled=True),
        lax.psum_scatter(partial_rows[2], "head", scatter_dimension=1, tiled=True),
        lax.psum_scatter(partial_rows[3], "head", scatter_dimension=1, tiled=True),
    )
    return (
        output,
        grad_inputs,
        summed[0],
        summed[1],
        summed[2],
        summed[3],
        finals[0],
        summed[4],
        finals[1],
        summed[5],
        finals[2],
        summed[6],
        finals[3],
        summed[5],
    )


def solution(mesh):
    return jax.shard_map(
        body,
        mesh=mesh,
        in_specs=(
            P(("dp", "head"), None),
            P("dp", None),
            P(),
            P(),
            P(),
            P(),
            P(),
            P(),
            P(),
            P(),
            P(),
            P(),
            P(),
            P(),
            P(("dp", "head"), None),
        ),
        out_specs=(
            P(("dp", "head"), None),
            P(("dp", "head"), None),
            P(),
            P(),
            P(),
            P(),
            P("dp", "head"),
            P(),
            P("dp", "head"),
            P(),
            P("dp", "head"),
            P(),
            P("dp", "head"),
            P(),
        ),
        check_vma=False,
    )
```

profile of v0, /device:TPU:0, one launch (start us, length us, event | category | flops | bytes accessed | tf_op | source)
XLA Modules:
  0.0 1508.9 jit_solution(16333594497788970276)
XLA Ops:
  12.6 8.4 add_convert_fusion.1
  25.6 6.6 copy.84
  40.9 45.1 %all-to-all-done = bf16[512,3,1024]{0,1,2:T(4,128)(2,1)} async-done(((bf16[512,3,1024]{0,1,2:T(4,128)(2,1)}), bf16[512,3,1024]{0,1,2:T(4,128)(2,1)}, u32[]{:S(2)}, u32[]{:S(2)}) %all-to-all-start) | async-done | bytes 3145760 | tf_op jit(solution)/shard_map/all_to_all | solution.py:100
  117.6 69.1 %while.27 = (s32[]{:T(128)}, bf16[4,512,4,64]{1,3,2,0:T(8,128)(2,1)}, f32[4,4,512]{2,1,0:T(4,128)S(1)}, s32[4]{0:T(128)S(1)}, s32[2048]{0:T(1024)S(1)}, /*index=...) while((s32[]{:T(128)}, ...), condition=%wide.region_8.9_spmd, body=%wide.region_5.0_spmd.sunk | while | flops 1127348736 | bytes 61426396 | solution.py:126
  146.2 5.9 fusion.136
  196.3 9.1 all-to-all-done.1
  210.3 306.1 %while.28 = (s32[]{:T(128)}, f32[2048,4,64]{0,2,1:T(8,128)}, f32[2048,4,64]{0,2,1:T(8,128)}, f32[4,512,4,64]{1,0,3,2:T(4,128)}, s32[4]{0:T(128)S(1)}, /*index=5*...) while((s32[]{:T(128)}, f32[2048,4,64]{0,2,1:T(8,128)}, ...), condition=%wide.region_11.12_spmd.clone, body=%wide.region_9.11_spmd.clone.sunk | while | flops 2753165824 | bytes 187246960 | solution.py:180
  214.2 9.2 fusion.146
  225.4 14.8 multiply_reduce_fusion.4
  240.2 12.4 multiply_convert_fusion.3
  257.1 11.1 dynamic_update_slice.20
  268.3 6.5 fusion.148
  274.8 12.1 fusion.149
  290.4 9.0 fusion.146
  301.4 14.8 multiply_reduce_fusion.4
  316.2 12.1 multiply_convert_fusion.3
  332.9 11.1 dynamic_update_slice.20
  344.0 7.1 fusion.148
  351.0 12.4 fusion.149
  366.9 9.0 fusion.146
  377.9 14.8 multiply_reduce_fusion.4
  392.6 12.1 multiply_convert_fusion.3
  409.3 11.1 dynamic_update_slice.20
  420.4 7.1 fusion.148
  427.4 12.4 fusion.149
  443.3 9.0 fusion.146
  454.3 14.8 multiply_reduce_fusion.4
  469.1 12.1 multiply_convert_fusion.3
  485.7 11.1 dynamic_update_slice.20
  496.8 7.1 fusion.148
  503.9 12.4 fusion.149
  528.4 7.2 copy.93
  535.6 51.9 %all_to_all.68 = bf16[2048,3,256]{2,1,0:T(4,128)(2,1)S(1)} all-to-all(bf16[2048,3,256]{2,1,0:T(4,128)(2,1)} %copy.93), channel_id=1, replica_groups=mesh['dp'=8,'head'=4] {'head'}, dimensions={0} | all-to-all | bytes 6291456 | tf_op jit(solution)/shard_map/all_to_all | solution.py:190
  595.3 8.7 fusion.75
  604.7 7.2 fusion.73
  612.0 28.6 %convert_reduce_fusion = (f32[4096]{0:T(1024)S(1)}, bf16[512,4096]{1,0:T(8,128)(2,1)}, f32[512,4096]{1,0:T(8,128)}) fusion(f32[512,4096]{1,0:T(8,128)S(1)} %fusion.73, f32[4096]{0:T(1024)S(1)} %convert_element_type.119, bf16[512,1024]{1,0:T(8,128)(2,1)S(1)} %copy-done.10, bf16[4096,1024]{1,0:T(8,128)(2,1)} %param.31), kind=kOutput, calls=%fused_computation.49 | convolution fusion | flops 4452249600 | bytes 30441472 | tf_op jit(solution)/shard_map/td,fd->tf/dot_general | solution.py:141
  640.6 10.0 multiply_convert_fusion.1
  650.6 10.8 fusion.83
  661.5 10.5 fusion.71
  672.6 140.0 %reduce-scatter.9.cloned.1.call-done = f32[128,3072]{1,0:T(8,128)} async-done(((f32[1024,3072]{1,0:T(8,128)}), f32[128,3072]{1,0:T(8,128)}) %reduce-scatter.9.cloned.1.call-update) | async-done | bytes 1572880 | tf_op jit(solution)/shard_map/reduce_scatter | solution.py:217
  812.7 282.6 %reduce-scatter.21.cloned.1.call-done = f32[512,1024]{1,0:T(8,128)} async-done(((f32[4096,1024]{1,0:T(8,128)}), f32[512,1024]{1,0:T(8,128)}) %reduce-scatter.21.cloned.1.call-update) | async-done | bytes 2097168 | tf_op jit(solution)/shard_map/reduce_scatter | solution.py:220
  1095.4 10.5 fusion.81
  1105.9 271.7 %reduce-scatter.17.cloned.1.call-done = f32[128,4096]{1,0:T(8,128)} async-done(((f32[1024,4096]{1,0:T(8,128)}), f32[128,4096]{1,0:T(8,128)}) %reduce-scatter.17.cloned.1.call-update) | async-done | bytes 2097168 | tf_op jit(solution)/shard_map/reduce_scatter | solution.py:219
  1377.6 8.4 fusion.80
  1390.0 7.0 fusion.65
  1399.5 40.4 %all-reduce = (f32[1024]{0:T(1024)}, f32[1024]{0:T(1024)}, f32[1024]{0:T(1024)}, f32[1024]{0:T(1024)}, f32[3072]{0:T(1024)}, /*index=5*/f32[1024]{0:T(1024)S(1)}, f32[4096]{0:T(1024)}) all-reduce(f32[1024]{0:T(1024)S(1)} %get-tuple-element.189, f32[1024]{0:T(1024)S(1)} %get-tuple-element.194, ...), channel_id=1, replica_groups=mesh['dp'=8,'head'=4] {'dp','head'}, use_global_device_ids=true, to_apply=%region_17.18 | all-reduce | flops 12288 | bytes 98304 | tf_op jit(solution)/shard_map/psum | solution.py:203
  1439.9 26.8 %reduce-scatter.23.cloned.1.call-done = f32[512,256]{1,0:T(8,128)} async-done(((f32[512,1024]{1,0:T(8,128)}), f32[512,256]{1,0:T(8,128)}) %reduce-scatter.23.cloned.1.call-update) | async-done | bytes 524304 | tf_op jit(solution)/shard_map/reduce_scatter | solution.py:226
  1466.7 34.3 %reduce-scatter.19.cloned.1.call-done = f32[128,1024]{1,0:T(8,128)} async-done(((f32[128,4096]{1,0:T(8,128)}), f32[128,1024]{1,0:T(8,128)}) %reduce-scatter.19.cloned.1.call-update) | async-done | bytes 524304 | tf_op jit(solution)/shard_map/reduce_scatter | solution.py:225
  (232 shorter events, 182.8 us)
Async XLA Ops:
  7.2 30.2 %copy-start = (bf16[1024,1024]{1,0:T(8,128)(2,1)S(1)}, bf16[1024,1024]{1,0:T(8,128)(2,1)}, u32[]{:S(2)}) copy-start(bf16[1024,1024]{1,0:T(8,128)(2,1)} %param.27) | copy-start | bytes 6291460
  8.8 3.7 copy-start.16
  32.1 5.0 copy-start.31
  32.1 5.2 copy-start.9
  32.1 53.9 %all-to-all-start = ((bf16[512,3,1024]{0,1,2:T(4,128)(2,1)}), bf16[512,3,1024]{0,1,2:T(4,128)(2,1)}, u32[]{:S(2)}, u32[]{:S(2)}) async-start(bf16[512,3,1024]{0,1,2:T(4,128)(2,1)} %copy.84), calls=%async_computation | async-start | bytes 8388608 | tf_op jit(solution)/shard_map/all_to_all | solution.py:100
  40.9 72.8 %copy-start.12 = (f32[2048,8]{0,1:T(8,128)}, f32[2048,8]{0,1:T(8,128)S(1)}, u32[]{:S(2)}) copy-start(f32[2048,8]{0,1:T(8,128)S(1)} %get-tuple-element.272) | copy-start | bytes 196612
  86.0 100.7 %all-to-all-start.2 = ((bf16[512,4,256]{2,0,1:T(8,128)(2,1)}), bf16[512,4,256]{2,0,1:T(8,128)(2,1)}, u32[]{:S(2)}, u32[]{:S(2)}) async-start(bf16[512,4,256]{2,0,1:T(8,128)(2,1)} %bitcast.89), calls=%async_computation.2 | async-start | bytes 2097152 | tf_op jit(solution)/shard_map/all_to_all | solution.py:149
  124.5 4.4 copy-start.4
  141.8 4.4 copy-start.4
  159.1 4.4 copy-start.4
  176.4 4.4 copy-start.4
  186.7 18.8 %all-to-all-start.1 = ((bf16[4,512,256]{1,2,0:T(8,128)(2,1)}), bf16[4,512,256]{1,2,0:T(8,128)(2,1)}, u32[]{:S(2)}, u32[]{:S(2)}) async-start(bf16[4,512,256]{1,2,0:T(8,128)(2,1)} %bitcast.15), calls=%async_computation.1 | async-start | bytes 2097152 | tf_op jit(solution)/shard_map/all_to_all | solution.py:128
  190.9 481.1 %reduce-scatter.13.cloned.1.call-start = ((), (), s32[]{:S(2)}) async-start(), calls=%async_computation.14 | async-start | bytes 4718592 | tf_op jit(solution)/shard_map/reduce_scatter | solution.py:218
  210.2 602.4 %reduce-scatter.9.cloned.1.call-start = ((), (), s32[]{:S(2)}) async-start(), calls=%async_computation.12 | async-start | bytes 14155776 | tf_op jit(solution)/shard_map/reduce_scatter | solution.py:217
  225.4 14.8 copy-start.2
  252.6 3.2 copy-start.1
  268.3 6.5 copy-start.3
  301.4 14.8 copy-start.2
  328.3 3.2 copy-start.1
  344.0 7.1 copy-start.3
  377.8 14.8 copy-start.2
  404.7 3.2 copy-start.1
  420.4 7.1 copy-start.3
  454.3 14.8 copy-start.2
  496.8 7.1 copy-start.3
  520.0 4.8 copy-start.13
  520.0 4.8 copy-start.14
  590.5 4.8 copy-start.5
  590.5 4.8 copy-start.17
  590.5 4.8 copy-start.19
  590.5 4.8 copy-start.22
  590.5 4.8 copy-start.25
  604.0 491.2 %reduce-scatter.21.cloned.1.call-start = ((), (), s32[]{:S(2)}) async-start(), calls=%async_computation.18 | async-start | bytes 18874368 | tf_op jit(solution)/shard_map/reduce_scatter | solution.py:220
  604.7 7.2 copy-start.10
  612.0 28.7 %copy-start.6 = (f32[512,4096]{1,0:T(8,128)}, f32[512,4096]{1,0:T(8,128)S(1)}, u32[]{:S(2)}) copy-start(f32[512,4096]{1,0:T(8,128)S(1)} %fusion.73) | copy-start | bytes 25165828
  661.5 716.1 %reduce-scatter.17.cloned.1.call-start = ((), (), s32[]{:S(2)}) async-start(), calls=%async_computation.16 | async-start | bytes 18874368 | tf_op jit(solution)/shard_map/reduce_scatter | solution.py:219
  672.0 423.4 %copy-start.29 = (bf16[1024]{0:T(1024)(128)(2,1)S(1)}, bf16[1024]{0:T(1024)(128)(2,1)}, u32[]{:S(2)}) copy-start(bf16[1024]{0:T(1024)(128)(2,1)} %param.28) | copy-start | bytes 6148
  672.0 423.4 %copy-start.30 = (bf16[1024]{0:T(1024)(128)(2,1)S(1)}, bf16[1024]{0:T(1024)(128)(2,1)}, u32[]{:S(2)}) copy-start(bf16[1024]{0:T(1024)(128)(2,1)} %param.32) | copy-start | bytes 6148
  672.0 767.9 %reduce-scatter.15.cloned.1.call-start = ((), (), s32[]{:S(2)}) async-start(), calls=%async_computation.15 | async-start | bytes 655360 | tf_op jit(solution)/shard_map/reduce_scatter | solution.py:224
  672.6 767.3 %reduce-scatter.11.cloned.1.call-start = ((), (), s32[]{:S(2)}) async-start(), calls=%async_computation.13 | async-start | bytes 1966080 | tf_op jit(solution)/shard_map/reduce_scatter | solution.py:223
  812.6 654.1 %reduce-scatter.23.cloned.1.call-start = ((), (), s32[]{:S(2)}) async-start(), calls=%async_computation.19 | async-start | bytes 2621440 | tf_op jit(solution)/shard_map/reduce_scatter | solution.py:226
  1095.3 405.7 %reduce-scatter.19.cloned.1.call-start = ((), (), s32[]{:S(2)}) async-start(), calls=%async_computation.17 | async-start | bytes 2621440 | tf_op jit(solution)/shard_map/reduce_scatter | solution.py:225
  1386.0 3.9 copy-start.15
  1386.0 3.9 copy-start.7
  1386.1 3.9 copy-start.8
  1386.1 3.9 copy-start.20
  1390.0 7.1 copy-start.11
  1439.9 61.7 %copy-start.26 = (f32[1024]{0:T(1024)}, f32[1024]{0:T(1024)S(1)}, u32[]{:S(2)}) copy-start(f32[1024]{0:T(1024)S(1)} %get-tuple-element.511) | copy-start | bytes 12292
  (7 other events, 9.5 us)
Sparse Core Ops, SparseCore 0:
  210.3 89.3 reduce-scatter.12
  604.2 208.3 reduce-scatter.8
  816.4 278.8 reduce-scatter.20
  1098.9 278.6 reduce-scatter.16
  1380.5 20.7 reduce-scatter.14
  1404.3 28.1 reduce-scatter.10
  1435.5 31.1 reduce-scatter.22
  1469.8 31.1 reduce-scatter.18
where the time goes:
time: 1520 us; the launch traced here: 1510 us
  waiting for transfers between devices  810 us (53%)
  matrix products  334 us (22%)
  local copies, waits for them, and re-layouts  115 us (8%)
  other arithmetic  114 us (8%)
  blocking collectives  92.3 us (6%)
    reduce_scatter x1, waiting for transfers between devices, body(): lax.psum_scatter(matrices[3], 'dp', scatter_dimension=0, tiled=True)  283 us
    reduce_scatter x1, waiting for transfers between devices, body(): lax.psum_scatter(matrices[2], 'dp', scatter_dimension=0, tiled=True)  272 us
    reduce_scatter x1, waiting for transfers between devices, body(): lax.psum_scatter(matrices[0], 'dp', scatter_dimension=0, tiled=True)  140 us
    dot_general x4, matrix products, backward_block(): jnp.einsum('qhd,khd->hqk', grad_out_blk, values, preferred_element_type=j...  59.1 us
    dot_general x8, matrix products, block_scores(): jnp.einsum('qhd,khd->hqk', query_blk, keys_rot, preferred_element_type=jn...  54.1 us
    all_to_all x1, blocking collectives, body(): lax.all_to_all(grad_heads, 'head', split_axis=0, concat_axis=2, tiled=True)  51.9 us
    dynamic_update_slice x8, local copies, waits for them, and re-layouts, body(): lax.scan(backward_block, (zeros_kv, zeros_kv), jnp.arange(blocks, dtype=j...  49.8 us
    dot_general x4, matrix products, backward_block(): jnp.einsum('hqk,qhd->khd', probs_low, grad_out_blk, preferred_element_typ...  49.2 us
  transfers between devices with their start and end apart: 11, of which 7 were waited for; matrix products, arithmetic and copies ran while one was open for 35% of the time, Pallas kernels for 0%

commit v1 on v0

--- a/solution.py
+++ b/solution.py
@@ -97,9 +97,20 @@
     triple = (
         jnp.dot(norm_attn, w_qkv, preferred_element_type=jnp.float32) + b_qkv.astype(jnp.float32)
     ).astype(jnp.bfloat16)
-    triple_heads = lax.all_to_all(
-        triple.reshape(tok_rows, 3, width), "head", split_axis=2, concat_axis=0, tiled=True
-    )
+    x = triple.reshape(tok_rows, 3, width)
+    ways, here = (lax.axis_size("head"), lax.axis_index("head"))
+    width_2 = x.shape[2] // ways
+    shape = list(x.shape)
+    shape[2] = width_2
+    height = shape[0]
+    shape[0] = height * ways
+    full = jnp.zeros(shape, x.dtype)
+    for mask in range(ways):
+        part = lax.dynamic_slice_in_dim(x, (here ^ mask) * width_2, width_2, axis=2)
+        if mask:
+            part = lax.ppermute(part, "head", [(d, d ^ mask) for d in range(ways)])
+        full = lax.dynamic_update_slice_in_dim(full, part, (here ^ mask) * height, axis=0)
+    triple_heads = full
     group_rows = triple_heads.shape[0]
     local_width = triple_heads.shape[2]
     local_heads = local_width // HD

time: 1520 us -> 1470 us (0.967)
  waiting for transfers between devices: 810 us -> 787 us
    all_to_all x1 -> x0, waiting for transfers between devices: 45.1 us -> none  [body(): lax.all_to_all(triple.reshape(tok_rows, 3, width), 'head', split_axis=2,...]
    ppermute x0 -> x3, waiting for transfers between devices: none -> 22.6 us  [body(): part = lax.ppermute(part, 'head', [(d, d ^ mask) for d in range(ways)])]
  transfers between devices with their start and end apart: 11 -> 13, of which waited for: 7 -> 8; matrix products, arithmetic and copies ran while one was open for 35% -> 35% of each run, Pallas kernels for 0% -> 0%
where the time goes in v1:
time: 1470 us
  waiting for transfers between devices  787 us (54%)
  matrix products  334 us (23%)
  other arithmetic  109 us (7%)
  local copies, waits for them, and re-layouts  101 us (7%)
  blocking collectives  92.3 us (6%)
  between operations  15.2 us (1%)
    reduce_scatter x1, waiting for transfers between devices, body(): lax.psum_scatter(matrices[3], 'dp', scatter_dimension=0, tiled=True)  283 us
    reduce_scatter x1, waiting for transfers between devices, body(): lax.psum_scatter(matrices[2], 'dp', scatter_dimension=0, tiled=True)  272 us
    reduce_scatter x1, waiting for transfers between devices, body(): lax.psum_scatter(matrices[0], 'dp', scatter_dimension=0, tiled=True)  139 us
    dot_general x4, matrix products, backward_block(): jnp.einsum('qhd,khd->hqk', grad_out_blk, values, preferred_element_type=j...  59.1 us
    dot_general x8, matrix products, block_scores(): jnp.einsum('qhd,khd->hqk', query_blk, keys_rot, preferred_element_type=jn...  53.9 us
    all_to_all x1, blocking collectives, body(): lax.all_to_all(grad_heads, 'head', split_axis=0, concat_axis=2, tiled=True)  51.9 us
    dynamic_update_slice x8, local copies, waits for them, and re-layouts, body(): lax.scan(backward_block, (zeros_kv, zeros_kv), jnp.arange(blocks, dtype=j...  49.8 us
    dot_general x4, matrix products, backward_block(): jnp.einsum('hqk,qhd->khd', probs_low, grad_out_blk, preferred_element_typ...  49.2 us
  transfers between devices with their start and end apart: 13, of which 8 were waited for; matrix products, arithmetic and copies ran while one was open for 35% of the time, Pallas kernels for 0%

profile of v1, /device:TPU:0, one launch (start us, length us, event | category | flops | bytes accessed | tf_op | source)
XLA Modules:
  0.0 1465.3 jit_solution(12182415208427848532)
XLA Ops:
  12.6 8.3 add_convert_fusion.1
  42.5 8.2 collective-permute-done.1
  52.8 14.4 collective-permute-done.2
  74.3 69.1 %while.27 = (s32[]{:T(128)}, bf16[4,512,4,64]{1,3,2,0:T(8,128)(2,1)}, f32[4,4,512]{2,1,0:T(4,128)S(1)}, s32[4]{0:T(128)S(1)}, s32[2048]{0:T(1024)S(1)}, /*index=...) while((s32[]{:T(128)}, ...), condition=%wide.region_8.9_spmd, body=%wide.region_5.0_spmd.sunk | while | flops 1127348736 | bytes 61426396 | solution.py:137
  85.7 5.9 fusion.136
  153.1 9.5 all-to-all-done
  167.4 306.0 %while.28 = (s32[]{:T(128)}, f32[2048,4,64]{0,2,1:T(8,128)}, f32[2048,4,64]{0,2,1:T(8,128)}, f32[4,512,4,64]{1,0,3,2:T(4,128)}, s32[4]{0:T(128)S(1)}, /*index=5*...) while((s32[]{:T(128)}, f32[2048,4,64]{0,2,1:T(8,128)}, ...), condition=%wide.region_11.12_spmd.clone, body=%wide.region_9.11_spmd.clone.sunk | while | flops 2753165824 | bytes 187246960 | solution.py:191
  171.4 9.0 fusion.146
  182.4 14.8 %multiply_reduce_fusion.4 = (f32[4,512]{1,0:T(4,128)S(1)}, f32[4,512,2048]{2,1,0:T(8,128)}) fusion(f32[4,512,2048]{2,1,0:T(8,128)} %fusion.146, f32[4,512]{1,0:T(4,128)S(1)} %dynamic-slice_bitcast_fusion.2, pred[512,2048]{1,0:T(8,128)(4,1)} %fusion.147, bf16[2048,4,64]{0,2,1:T(8,128)(2,1)} %get-tuple-element.463, ...), kind=kOutput, calls=%fused_computation.19.clone.1 | convolution fusion | flops 557840384 | bytes 35930116 | tf_op jit(solution)/shard_map/while/body/eval_jaxpr/qhd,khd->hqk/dot_general | solution.py:174
  197.2 12.4 multiply_convert_fusion.3
  214.1 11.1 dynamic_update_slice.40
  225.3 6.6 fusion.148
  231.8 12.1 fusion.149
  247.5 9.0 fusion.146
  258.5 14.8 %multiply_reduce_fusion.4 = (f32[4,512]{1,0:T(4,128)S(1)}, f32[4,512,2048]{2,1,0:T(8,128)}) fusion(f32[4,512,2048]{2,1,0:T(8,128)} %fusion.146, f32[4,512]{1,0:T(4,128)S(1)} %dynamic-slice_bitcast_fusion.2, pred[512,2048]{1,0:T(8,128)(4,1)} %fusion.147, bf16[2048,4,64]{0,2,1:T(8,128)(2,1)} %get-tuple-element.463, ...), kind=kOutput, calls=%fused_computation.19.clone.1 | convolution fusion | flops 557840384 | bytes 35930116 | tf_op jit(solution)/shard_map/while/body/eval_jaxpr/qhd,khd->hqk/dot_general | solution.py:174
  273.2 12.1 multiply_convert_fusion.3
  289.9 11.1 dynamic_update_slice.40
  301.0 7.1 fusion.148
  308.0 12.4 fusion.149
  323.9 9.0 fusion.146
  334.9 14.8 %multiply_reduce_fusion.4 = (f32[4,512]{1,0:T(4,128)S(1)}, f32[4,512,2048]{2,1,0:T(8,128)}) fusion(f32[4,512,2048]{2,1,0:T(8,128)} %fusion.146, f32[4,512]{1,0:T(4,128)S(1)} %dynamic-slice_bitcast_fusion.2, pred[512,2048]{1,0:T(8,128)(4,1)} %fusion.147, bf16[2048,4,64]{0,2,1:T(8,128)(2,1)} %get-tuple-element.463, ...), kind=kOutput, calls=%fused_computation.19.clone.1 | convolution fusion | flops 557840384 | bytes 35930116 | tf_op jit(solution)/shard_map/while/body/eval_jaxpr/qhd,khd->hqk/dot_general | solution.py:174
  349.7 12.1 multiply_convert_fusion.3
  366.3 11.1 dynamic_update_slice.40
  377.4 7.1 fusion.148
  384.5 12.4 fusion.149
  400.3 9.0 fusion.146
  411.3 14.8 %multiply_reduce_fusion.4 = (f32[4,512]{1,0:T(4,128)S(1)}, f32[4,512,2048]{2,1,0:T(8,128)}) fusion(f32[4,512,2048]{2,1,0:T(8,128)} %fusion.146, f32[4,512]{1,0:T(4,128)S(1)} %dynamic-slice_bitcast_fusion.2, pred[512,2048]{1,0:T(8,128)(4,1)} %fusion.147, bf16[2048,4,64]{0,2,1:T(8,128)(2,1)} %get-tuple-element.463, ...), kind=kOutput, calls=%fused_computation.19.clone.1 | convolution fusion | flops 557840384 | bytes 35930116 | tf_op jit(solution)/shard_map/while/body/eval_jaxpr/qhd,khd->hqk/dot_general | solution.py:174
  426.1 12.1 multiply_convert_fusion.3
  442.8 11.1 dynamic_update_slice.40
  453.9 7.1 fusion.148
  460.9 12.4 fusion.149
  485.4 7.2 copy.67
  492.6 51.9 %all_to_all.50 = bf16[2048,3,256]{2,1,0:T(4,128)(2,1)S(1)} all-to-all(bf16[2048,3,256]{2,1,0:T(4,128)(2,1)} %copy.67), channel_id=1, replica_groups=mesh['dp'=8,'head'=4] {'head'}, dimensions={0} | all-to-all | bytes 6291456 | tf_op jit(solution)/shard_map/all_to_all | solution.py:201
  552.3 8.7 fusion.75
  561.8 7.2 fusion.73
  569.0 28.6 %convert_reduce_fusion = (f32[4096]{0:T(1024)S(1)}, bf16[512,4096]{1,0:T(8,128)(2,1)}, f32[512,4096]{1,0:T(8,128)}) fusion(f32[512,4096]{1,0:T(8,128)S(1)} %fusion.73, f32[4096]{0:T(1024)S(1)} %convert_element_type.119, bf16[512,1024]{1,0:T(8,128)(2,1)S(1)} %copy-done.12, bf16[4096,1024]{1,0:T(8,128)(2,1)} %param.31), kind=kOutput, calls=%fused_computation.49 | convolution fusion | flops 4452249600 | bytes 30441472 | tf_op jit(solution)/shard_map/td,fd->tf/dot_general | solution.py:152
  597.6 10.0 multiply_convert_fusion.1
  607.6 10.8 fusion.83
  618.5 10.6 fusion.71
  629.8 139.3 %reduce-scatter.9.cloned.1.call-done = f32[128,3072]{1,0:T(8,128)} async-done(((f32[1024,3072]{1,0:T(8,128)}), f32[128,3072]{1,0:T(8,128)}) %reduce-scatter.9.cloned.1.call-update) | async-done | bytes 1572880 | tf_op jit(solution)/shard_map/reduce_scatter | solution.py:228
  769.1 282.6 %reduce-scatter.21.cloned.1.call-done = f32[512,1024]{1,0:T(8,128)} async-done(((f32[4096,1024]{1,0:T(8,128)}), f32[512,1024]{1,0:T(8,128)}) %reduce-scatter.21.cloned.1.call-update) | async-done | bytes 2097168 | tf_op jit(solution)/shard_map/reduce_scatter | solution.py:231
  1051.8 10.5 fusion.81
  1062.3 271.7 %reduce-scatter.17.cloned.1.call-done = f32[128,4096]{1,0:T(8,128)} async-done(((f32[1024,4096]{1,0:T(8,128)}), f32[128,4096]{1,0:T(8,128)}) %reduce-scatter.17.cloned.1.call-update) | async-done | bytes 2097168 | tf_op jit(solution)/shard_map/reduce_scatter | solution.py:230
  1334.0 8.4 fusion.80
  1346.3 7.0 fusion.65
  1355.8 40.4 %all-reduce = (f32[1024]{0:T(1024)}, f32[1024]{0:T(1024)}, f32[1024]{0:T(1024)}, f32[1024]{0:T(1024)}, f32[3072]{0:T(1024)}, /*index=5*/f32[1024]{0:T(1024)S(1)}, f32[4096]{0:T(1024)}) all-reduce(f32[1024]{0:T(1024)S(1)} %get-tuple-element.170, f32[1024]{0:T(1024)S(1)} %get-tuple-element.175, ...), channel_id=1, replica_groups=mesh['dp'=8,'head'=4] {'dp','head'}, use_global_device_ids=true, to_apply=%region_17.18 | all-reduce | flops 12288 | bytes 98304 | tf_op jit(solution)/shard_map/psum | solution.py:214
  1396.3 26.8 %reduce-scatter.23.cloned.1.call-done = f32[512,256]{1,0:T(8,128)} async-done(((f32[512,1024]{1,0:T(8,128)}), f32[512,256]{1,0:T(8,128)}) %reduce-scatter.23.cloned.1.call-update) | async-done | bytes 524304 | tf_op jit(solution)/shard_map/reduce_scatter | solution.py:237
  1423.1 34.3 %reduce-scatter.19.cloned.1.call-done = f32[128,1024]{1,0:T(8,128)} async-done(((f32[128,4096]{1,0:T(8,128)}), f32[128,1024]{1,0:T(8,128)}) %reduce-scatter.19.cloned.1.call-update) | async-done | bytes 524304 | tf_op jit(solution)/shard_map/reduce_scatter | solution.py:236
  (239 shorter events, 168.6 us)
Async XLA Ops:
  7.2 24.9 %copy-start = (bf16[1024,1024]{1,0:T(8,128)(2,1)S(1)}, bf16[1024,1024]{1,0:T(8,128)(2,1)}, u32[]{:S(2)}) copy-start(bf16[1024,1024]{1,0:T(8,128)(2,1)} %param.27) | copy-start | bytes 6291460
  8.8 3.7 copy-start.18
  25.6 6.5 copy-start.11
  28.9 4.4 copy-start.6
  28.9 11.4 collective-permute-start
  29.4 21.2 %collective-permute-start.1 = (bf16[512,3,256]{0,2,1:T(8,128)(2,1)}, bf16[512,3,256]{0,2,1:T(8,128)(2,1)}, u32[]{:S(2)}, u32[]{:S(2)}) collective-permute-start(bf16[512,3,256]{0,2,1:T(8,128)(2,1)} %get-tuple-element.238), channel_id=1, source_target_pairs={{0,2},{1,3},{2,0},{3,1},{4,6},{5,7},{6,4},{7,5},{8,10},{9,11},{10,... | collective-permute-start | bytes 2359304 | tf_op jit(solution)/shard_map/ppermute | solution.py:111
  31.9 35.2 %collective-permute-start.2 = (bf16[512,3,256]{0,2,1:T(8,128)(2,1)S(1)}, bf16[512,3,256]{0,2,1:T(8,128)(2,1)}, u32[]{:S(2)}, u32[]{:S(2)}) collective-permute-start(bf16[512,3,256]{0,2,1:T(8,128)(2,1)S(1)} %get-tuple-element.237), channel_id=1, source_target_pairs={{0,3},{1,2},{2,1},{3,0},{4,7},{5,6},{6,5},{7,4},{8,11},{9,10},{10,... | collective-permute-start | bytes 2359304 | tf_op jit(solution)/shard_map/ppermute | solution.py:111
  33.4 5.5 copy-start.33
  34.4 109.0 %all-to-all-start.1 = ((bf16[512,4,256]{2,0,1:T(8,128)(2,1)}), bf16[512,4,256]{2,0,1:T(8,128)(2,1)}, u32[]{:S(2)}, u32[]{:S(2)}) async-start(bf16[512,4,256]{2,0,1:T(8,128)(2,1)} %bitcast.85), calls=%async_computation.1 | async-start | bytes 2097152 | tf_op jit(solution)/shard_map/all_to_all | solution.py:160
  40.3 32.8 %copy-start.14 = (f32[2048,8]{0,1:T(8,128)}, f32[2048,8]{0,1:T(8,128)S(1)}, u32[]{:S(2)}) copy-start(f32[2048,8]{0,1:T(8,128)S(1)} %get-tuple-element.257) | copy-start | bytes 196612
  81.3 4.4 copy-start.4
  98.6 4.4 copy-start.4
  115.9 4.4 copy-start.4
  133.2 4.4 copy-start.4
  143.5 19.1 %all-to-all-start = ((bf16[4,512,256]{1,2,0:T(8,128)(2,1)}), bf16[4,512,256]{1,2,0:T(8,128)(2,1)}, u32[]{:S(2)}, u32[]{:S(2)}) async-start(bf16[4,512,256]{1,2,0:T(8,128)(2,1)} %bitcast.12), calls=%async_computation | async-start | bytes 2097152 | tf_op jit(solution)/shard_map/all_to_all | solution.py:139
  147.7 481.4 %reduce-scatter.13.cloned.1.call-start = ((), (), s32[]{:S(2)}) async-start(), calls=%async_computation.13 | async-start | bytes 4718592 | tf_op jit(solution)/shard_map/reduce_scatter | solution.py:229
  167.4 601.6 %reduce-scatter.9.cloned.1.call-start = ((), (), s32[]{:S(2)}) async-start(), calls=%async_computation.11 | async-start | bytes 14155776 | tf_op jit(solution)/shard_map/reduce_scatter | solution.py:228
  182.4 14.8 %copy-start.2 = (pred[512,2048]{1,0:T(8,128)(4,1)S(1)}, pred[512,2048]{1,0:T(8,128)(4,1)}, u32[]{:S(2)}) copy-start(pred[512,2048]{1,0:T(8,128)(4,1)} %fusion.147) | copy-start | bytes 3145732 | tf_op jit(solution)/shard_map/while
  225.3 6.6 copy-start.3
  258.4 14.8 %copy-start.2 = (pred[512,2048]{1,0:T(8,128)(4,1)S(1)}, pred[512,2048]{1,0:T(8,128)(4,1)}, u32[]{:S(2)}) copy-start(pred[512,2048]{1,0:T(8,128)(4,1)} %fusion.147) | copy-start | bytes 3145732 | tf_op jit(solution)/shard_map/while
  301.0 7.1 copy-start.3
  334.9 14.8 %copy-start.2 = (pred[512,2048]{1,0:T(8,128)(4,1)S(1)}, pred[512,2048]{1,0:T(8,128)(4,1)}, u32[]{:S(2)}) copy-start(pred[512,2048]{1,0:T(8,128)(4,1)} %fusion.147) | copy-start | bytes 3145732 | tf_op jit(solution)/shard_map/while
  377.4 7.1 copy-start.3
  411.3 14.8 %copy-start.2 = (pred[512,2048]{1,0:T(8,128)(4,1)S(1)}, pred[512,2048]{1,0:T(8,128)(4,1)}, u32[]{:S(2)}) copy-start(pred[512,2048]{1,0:T(8,128)(4,1)} %fusion.147) | copy-start | bytes 3145732 | tf_op jit(solution)/shard_map/while
  453.9 7.1 copy-start.3
  477.1 4.8 copy-start.15
  477.1 4.8 copy-start.16
  547.5 4.8 copy-start.7
  547.5 4.8 copy-start.19
  547.5 4.8 copy-start.21
  547.5 4.8 copy-start.24
  547.5 4.8 copy-start.27
  561.1 490.6 %reduce-scatter.21.cloned.1.call-start = ((), (), s32[]{:S(2)}) async-start(), calls=%async_computation.17 | async-start | bytes 18874368 | tf_op jit(solution)/shard_map/reduce_scatter | solution.py:231
  561.8 7.2 copy-start.12
  569.0 28.6 %copy-start.8 = (f32[512,4096]{1,0:T(8,128)}, f32[512,4096]{1,0:T(8,128)S(1)}, u32[]{:S(2)}) copy-start(f32[512,4096]{1,0:T(8,128)S(1)} %fusion.73) | copy-start | bytes 25165828
  618.5 715.5 %reduce-scatter.17.cloned.1.call-start = ((), (), s32[]{:S(2)}) async-start(), calls=%async_computation.15 | async-start | bytes 18874368 | tf_op jit(solution)/shard_map/reduce_scatter | solution.py:230
  629.1 422.7 %copy-start.31 = (bf16[1024]{0:T(1024)(128)(2,1)S(1)}, bf16[1024]{0:T(1024)(128)(2,1)}, u32[]{:S(2)}) copy-start(bf16[1024]{0:T(1024)(128)(2,1)} %param.28) | copy-start | bytes 6148
  629.1 422.7 %copy-start.32 = (bf16[1024]{0:T(1024)(128)(2,1)S(1)}, bf16[1024]{0:T(1024)(128)(2,1)}, u32[]{:S(2)}) copy-start(bf16[1024]{0:T(1024)(128)(2,1)} %param.32) | copy-start | bytes 6148
  629.1 767.2 %reduce-scatter.15.cloned.1.call-start = ((), (), s32[]{:S(2)}) async-start(), calls=%async_computation.14 | async-start | bytes 655360 | tf_op jit(solution)/shard_map/reduce_scatter | solution.py:235
  629.7 766.6 %reduce-scatter.11.cloned.1.call-start = ((), (), s32[]{:S(2)}) async-start(), calls=%async_computation.12 | async-start | bytes 1966080 | tf_op jit(solution)/shard_map/reduce_scatter | solution.py:234
  769.0 654.1 %reduce-scatter.23.cloned.1.call-start = ((), (), s32[]{:S(2)}) async-start(), calls=%async_computation.18 | async-start | bytes 2621440 | tf_op jit(solution)/shard_map/reduce_scatter | solution.py:237
  1051.7 405.7 %reduce-scatter.19.cloned.1.call-start = ((), (), s32[]{:S(2)}) async-start(), calls=%async_computation.16 | async-start | bytes 2621440 | tf_op jit(solution)/shard_map/reduce_scatter | solution.py:236
  1342.4 3.9 copy-start.17
  1342.4 3.9 copy-start.9
  1342.4 3.9 copy-start.10
  1342.5 3.9 copy-start.22
  1346.3 7.1 copy-start.13
  1396.3 61.8 %copy-start.28 = (f32[1024]{0:T(1024)}, f32[1024]{0:T(1024)S(1)}, u32[]{:S(2)}) copy-start(f32[1024]{0:T(1024)S(1)} %get-tuple-element.496) | copy-start | bytes 12292
  (11 other events, 21.1 us)
Sparse Core Ops, SparseCore 0:
  167.5 88.6 reduce-scatter.12
  561.2 207.7 reduce-scatter.8
  772.8 278.8 reduce-scatter.20
  1055.3 278.5 reduce-scatter.16
  1336.9 20.7 reduce-scatter.14
  1360.6 28.1 reduce-scatter.10
  1391.9 31.1 reduce-scatter.22
  1426.2 31.1 reduce-scatter.18
